TPU v7x, 32 devices: a whole 2x2x4 slice. The times are simulated.
32 devices in a mesh: groups: 2 (over x), ctx: 16 (over z, y, core).
Axes of the slice: x: 2, y: 2, z: 4, core: 2. Of those that a mesh axis runs over, the one named last changes fastest.
Arguments:
- queries: bfloat16 [512, 128, 576], P(('groups', 'ctx')), parts along dimension 0, may hold values from -4 to 4
- latent_cache: bfloat16 [32768, 576], P(('groups', 'ctx')), parts along dimension 0, may hold values from -4 to 4
- block_picks: int32 [32, 32], P(('groups', 'ctx')), parts along dimension 0, may hold values from 0 to 255, as said below
- lengths: int32 [512], P(('groups', 'ctx')), parts along dimension 0, may hold values from 8192 to 16384
Outputs:
- latent_out: bfloat16 [512, 128, 512], P(('groups', 'ctx')), parts along dimension 0
There are 2 independent parts, one for each index of `groups`. A program takes and returns all parts, laid end to end along the dimension named above; each array names one. Nothing has to cross between parts.
Inputs may be any that keep to these rules, and one draw needn't show every extreme that they name: `block_picks`: each row names 32 different blocks. At most 4 of a row's blocks lie in one owner's range of 16 consecutive blocks, and every row reaches this with its first 4 entries, which lie in the first half of the context. Over all rows together at most 8 different blocks of one owner's range are named, and some owner reaches this.
All inputs are finite; a program needn't handle non-finite values.
Results may differ from a plain program's by a relative error of at most 0.0035.
Values may be sent and summed in bfloat16 or wider, within the bound.
A program may use at most 128 MiB of HBM per device.

v0:
```python
import functools

import jax
import jax.numpy as jnp
from jax import lax
from jax.experimental import pallas as pl
from jax.experimental.pallas import tpu as pltpu
from jax.sharding import PartitionSpec as P

LAT = 512
BLOCK = 64
TOPK = 32
LANES = 128

SOFTMAX_SCALE = 192.0 ** (-0.5)
LOG2E = 1.4426950408889634
MESH = pl.DeviceIdType.MESH
HIDDEN = -1e30


def step_kernel(
    ctx_count, owned, units, picks_ref, lengths_ref, queries_ref, cache_ref, out_ref,
    raw_q, near_cache, q_ref, flags_ref, all_flags, gath, pool, keys_t, values, positions, order,
    top_ref, total_ref, acc_ref, q_sem, cache_sem, flag_send, flag_recv, send, recv,
):
    rows, feature, heads = queries_ref.shape
    rope = feature - LAT
    pair = 2 * BLOCK
    tall = pair * rope // LAT
    line = ctx_count // 4
    late_blocks = 4 * units
    early_blocks = TOPK - late_blocks
    me = lax.axis_index("ctx")
    core = lax.rem(me, 2)
    y = lax.rem(me // 2, 2)
    z = me // 4
    far = jnp.where(2 * z < line, line - 1, 0)

    fetch = pltpu.make_async_copy(queries_ref, raw_q, q_sem)
    fetch_cache = pltpu.make_async_copy(cache_ref, near_cache, cache_sem)
    fetch_cache.start()
    fetch.start()

    def at(zz, yy, cc):
        return (zz * 2 + yy) * 2 + cc

    barrier = pltpu.get_barrier_semaphore()

    @pl.loop(1, ctx_count)
    def _(d):
        pl.semaphore_signal(
            barrier, inc=1, device_id={"ctx": lax.rem(me + d, ctx_count)}, device_id_type=MESH
        )

    flag_rows = flags_ref.shape[0]
    block_id = lax.broadcasted_iota(jnp.int32, (flag_rows, LANES), 0) * LANES
    block_id += lax.broadcasted_iota(jnp.int32, (flag_rows, LANES), 1)
    lane = lax.broadcasted_iota(jnp.int32, (1, LANES), 1)
    flags = jnp.zeros((flag_rows, LANES), jnp.int32)
    ordered = jnp.zeros((1, LANES), jnp.int32)
    early_seen = jnp.int32(0)
    for k in range(TOPK):
        p = picks_ref[0, k]
        owner = p // owned
        is_late = owner // 4 == far
        place = jnp.where(is_late, TOPK - 1 - (k - early_seen), early_seen)
        early_seen += jnp.where(is_late, 0, 1)
        flags = jnp.where(block_id == p, 1, flags)
        ordered = jnp.where(lane == place, p, ordered)
    flags_ref[...] = flags

    pl.semaphore_wait(barrier, ctx_count - 1)

    def flag_copy(d):
        return pltpu.make_async_remote_copy(
            src_ref=flags_ref,
            dst_ref=all_flags.at[me],
            send_sem=flag_send.at[d],
            recv_sem=flag_recv.at[me],
            device_id={"ctx": lax.rem(me + d, ctx_count)},
            device_id_type=MESH,
        )

    def flag_arrival(source):
        return pltpu.make_async_remote_copy(
            src_ref=flags_ref,
            dst_ref=all_flags.at[source],
            send_sem=flag_send.at[0],
            recv_sem=flag_recv.at[source],
            device_id={"ctx": source},
            device_id_type=MESH,
        )

    @pl.loop(1, ctx_count)
    def _(d):
        flag_copy(d).start()

    all_flags[me] = flags

    @pl.loop(1, ctx_count)
    def _(d):
        flag_arrival(lax.rem(me + d, ctx_count)).wait_recv()

    named = jnp.minimum(jnp.max(all_flags[...], axis=0), 1)
    mine = (named > 0) & (block_id // owned == me)

    def unit_copy(slot, local, way, target):
        return pltpu.make_async_remote_copy(
            src_ref=gath.at[slot],
            dst_ref=gath.at[slot],
            send_sem=send.at[local, way],
            recv_sem=recv.at[slot],
            device_id={"ctx": target},
            device_id_type=MESH,
        )

    def slot_of(zz, j):
        crossed = (j == units).astype(jnp.int32)
        yy = lax.rem(y + crossed, 2)
        u = j * (1 - crossed)
        return at(zz, yy, core) * units + u, (zz * 2 + yy) * units + u

    up = at(lax.rem(z + 1, line), y, core)
    down = at(lax.rem(z + line - 1, line), y, core)
    across = at(z, 1 - y, core)
    sibling = at(z, y, 1 - core)

    def sends(zz, j):
        valid = (zz >= 0) & (zz < line) & ((j < units) | (core == 1))
        own_line = j < units
        return (
            (0, up, valid & (zz <= z) & (z + 1 < line)),
            (1, down, valid & (zz >= z) & (z > 0)),
            (2, across, valid & own_line & ((zz == z) | (core == 0) | (j > 0))),
            (3, sibling, valid),
        )

    def forward(zz, j, skip=()):
        slot, local = slot_of(zz, j)
        for way, target, yes in sends(zz, j):
            if way not in skip:
                @pl.when(yes)
                def _():
                    unit_copy(slot, local, way, target).start()

    def arrived(slot):
        unit_copy(slot, 0, 0, sibling).wait_recv()

    past = ctx_count * owned
    fetch_cache.wait()
    last = jnp.int32(-1)
    token = lax.broadcasted_iota(jnp.int32, (pair, owned * BLOCK), 0)
    column = lax.broadcasted_iota(jnp.int32, (pair, owned * BLOCK), 1)
    for u in range(units):
        starts = []
        for h in range(2):
            last = jnp.min(jnp.where(mine & (block_id > last), block_id, past))
            starts.append(jnp.minimum(last - me * owned, owned - 1) * BLOCK)
        wanted = jnp.where(token < BLOCK, starts[0] + token, starts[1] + token - BLOCK)
        chosen = jnp.where(column == wanted, 1.0, 0.0).astype(jnp.bfloat16)
        tokens = lax.dot_general(
            chosen, near_cache[...], (((1,), (1,)), ((), ())), preferred_element_type=jnp.float32
        ).astype(jnp.bfloat16)
        tail = tokens[:, LAT:]
        packed = jnp.concatenate(
            [tail[i * tall : (i + 1) * tall, :] for i in range(pair // tall)], axis=1
        )
        gath[me * units + u, :pair, :] = tokens[:, :LAT]
        gath[me * units + u, pair:, :] = packed
        pool[me * units + u, :pair, :] = tokens[:, :LAT]
        pool[me * units + u, pair:, :] = packed
        forward(z, jnp.int32(u))

    def keep(slot):
        pool[slot] = gath[slot]

    fetch.wait()

    def turn(row):
        q_ref[row] = raw_q[row].T

    for k in range(TOPK):
        order[k] = jnp.sum(jnp.where(lane == k, ordered, 0))

    per = units + 1

    def along(k):
        step = k // per
        j = lax.rem(k, per)
        for zz in (z + 1 + step, z - 1 - step):
            @pl.when((zz >= 0) & (zz < line) & ((j < units) | (core == 1)))
            def _():
                slot, _ = slot_of(zz, j)
                arrived(slot)
                forward(zz, j)
                keep(slot)

    main = per * (line - 2)

    @pl.loop(0, main)
    def _(k):
        along(k)

        @pl.when((k == 0) & (core == 1))
        def _():
            slot, _ = slot_of(z, jnp.int32(units))
            arrived(slot)
            forward(z, jnp.int32(units))
            keep(slot)

        @pl.when(k < rows)
        def _():
            turn(lax.rem(k, rows))

    @pl.loop(min(rows, main), rows)
    def _(row):
        turn(row)

    def cross(zz, j):
        @pl.when((core == 0) | (j > 0))
        def _():
            slot = at(zz, 1 - y, core) * units + j
            local = (zz * 2 + 1 - y) * units + j
            arrived(slot)
            unit_copy(slot, local, 3, sibling).start()
            keep(slot)

    def beside(owner, u):
        slot = owner * units + u
        arrived(slot)
        keep(slot)

    @pl.loop(0, units * line)
    def _(k):
        zz = lax.rem(z + k // units, line)

        @pl.when(k // units == line - 2)
        def _():
            along(main + lax.rem(k, units))

        @pl.when(zz != far)
        def _():
            cross(zz, lax.rem(k, units))

    @pl.loop(0, line * 2 * units)
    def _(k):
        o = k // units

        @pl.when(o // 2 != far)
        def _():
            beside(o * 2 + 1 - core, lax.rem(k, units))

    def fill(first_block, blocks):
        for k in range(first_block, first_block + blocks, 2):
            latent, tails, places = [], [], []
            for h in range(2):
                p = order[k + h]
                owner = p // owned
                slot = jnp.sum(jnp.where((block_id // owned == owner) & (block_id < p), named, 0))
                unit = pool[owner * units + slot // 2]
                first = lax.rem(slot, 2) == 0
                latent.append(jnp.where(first, unit[:BLOCK], unit[BLOCK:pair]))
                tail = jnp.where(first, unit[pair:, : LAT // 2], unit[pair:, LAT // 2 :])
                tails += [tail[:, i * rope : (i + 1) * rope] for i in range(BLOCK // tall)]
                places.append(p * BLOCK)
            latent = jnp.concatenate(latent, axis=0)
            tails = jnp.concatenate(tails, axis=0)
            span = slice(k * BLOCK, (k + 2) * BLOCK)
            values[span, :] = latent
            keys_t[:LAT, span] = latent.T
            keys_t[LAT:, span] = tails.T
            positions[:, span] = jnp.where(lane < BLOCK, places[0] + lane, places[1] + lane - BLOCK)

    scale = SOFTMAX_SCALE * LOG2E
    merged = 2 if rows % 4 == 0 else 1
    groups = rows // 2 // merged

    def scores(i, span):
        q = q_ref[pl.ds(2 * i, 2)].reshape(2 * heads, feature)
        s = jnp.dot(q, keys_t[:, span], preferred_element_type=jnp.float32)
        where = positions[:, span]
        return jnp.concatenate(
            [
                jnp.where(where < lengths_ref[2 * i + r], s[r * heads : (r + 1) * heads], HIDDEN)
                for r in range(2)
            ],
            axis=0,
        )

    early = slice(0, early_blocks * BLOCK)
    late = slice(early_blocks * BLOCK, TOPK * BLOCK)
    fill(0, early_blocks)

    @pl.loop(0, groups)
    def _(g):
        for m in range(merged):
            i = g * merged + m
            s = scores(i, early)
            top = jnp.max(s, axis=1, keepdims=True)
            e = jnp.exp2((s - top) * scale)
            top_ref[i] = top
            total_ref[i] = jnp.sum(e, axis=1, keepdims=True)
            acc_ref[i] = jnp.dot(
                e.astype(jnp.bfloat16), values[early, :], preferred_element_type=jnp.float32
            )

        @pl.when(g < units)
        def _():
            cross(far, g)

    @pl.loop(min(units, groups), units)
    def _(u):
        cross(far, u)

    along(jnp.int32(main + units))

    @pl.loop(0, 2 * units)
    def _(k):
        beside(at(far, k // units, 1 - core), lax.rem(k, units))

    fill(early_blocks, late_blocks)

    @pl.loop(0, groups)
    def _(g):
        for m in range(merged):
            i = g * merged + m
            s = scores(i, late)
            before = top_ref[i]
            top = jnp.maximum(before, jnp.max(s, axis=1, keepdims=True))
            e = jnp.exp2((s - top) * scale)
            shrink = jnp.exp2((before - top) * scale)
            total = total_ref[i] * shrink + jnp.sum(e, axis=1, keepdims=True)
            o = acc_ref[i] * shrink + jnp.dot(
                e.astype(jnp.bfloat16), values[late, :], preferred_element_type=jnp.float32
            )
            out_ref[pl.ds(2 * i, 2)] = (o / total).astype(jnp.bfloat16).reshape(2, heads, LAT)

    @pl.loop(1, ctx_count)
    def _(d):
        flag_copy(d).wait_send()

    @pl.loop(0, per * line)
    def _(k):
        zz = k // per
        j = lax.rem(k, per)
        slot, local = slot_of(zz, j)
        for way, target, yes in sends(zz, j):
            @pl.when(yes)
            def _():
                unit_copy(slot, local, way, target).wait_send()

    @pl.loop(0, units * line)
    def _(k):
        zz = k // units
        j = lax.rem(k, units)

        @pl.when((core == 0) | (j > 0))
        def _():
            slot = at(zz, 1 - y, core) * units + j
            local = (zz * 2 + 1 - y) * units + j
            unit_copy(slot, local, 3, sibling).wait_send()


def shards(queries, latent_cache, block_picks, lengths):
    ctx_count = lax.axis_size("ctx")
    rows, heads, feature = queries.shape
    owned = latent_cache.shape[0] // BLOCK
    units = max(1, 2 * TOPK // ctx_count)
    flag_rows = -(-(ctx_count * owned) // LANES // 8) * 8
    tall = 2 * BLOCK + 2 * BLOCK * (feature - LAT) // LAT
    keys = TOPK * BLOCK
    return pl.pallas_call(
        functools.partial(step_kernel, ctx_count, owned, units),
        out_shape=jax.ShapeDtypeStruct((rows, heads, LAT), jnp.bfloat16),
        in_specs=[
            pl.BlockSpec(memory_space=pltpu.SMEM),
            pl.BlockSpec(memory_space=pltpu.SMEM),
            pl.BlockSpec(memory_space=pl.ANY),
            pl.BlockSpec(memory_space=pl.ANY),
        ],
        out_specs=pl.BlockSpec(memory_space=pltpu.VMEM),
        scratch_shapes=[
            pltpu.VMEM((rows, feature, heads), jnp.bfloat16),
            pltpu.VMEM((feature, owned * BLOCK), jnp.bfloat16),
            pltpu.VMEM((rows, heads, feature), jnp.bfloat16),
            pltpu.VMEM((flag_rows, LANES), jnp.int32),
            pltpu.VMEM((ctx_count, flag_rows, LANES), jnp.int32),
            pltpu.VMEM((ctx_count * units, tall, LAT), jnp.bfloat16),
            pltpu.VMEM((ctx_count * units, tall, LAT), jnp.bfloat16),
            pltpu.VMEM((feature, keys), jnp.bfloat16),
            pltpu.VMEM((keys, LAT), jnp.bfloat16),
            pltpu.VMEM((1, keys), jnp.int32),
            pltpu.SMEM((TOPK,), jnp.int32),
            pltpu.VMEM((rows // 2, 2 * heads, 1), jnp.float32),
            pltpu.VMEM((rows // 2, 2 * heads, 1), jnp.float32),
            pltpu.VMEM((rows // 2, 2 * heads, LAT), jnp.float32),
            pltpu.SemaphoreType.DMA,
            pltpu.SemaphoreType.DMA,
            pltpu.SemaphoreType.DMA((ctx_count,)),
            pltpu.SemaphoreType.DMA((ctx_count,)),
            pltpu.SemaphoreType.DMA((ctx_count // 2 * units, 4)),
            pltpu.SemaphoreType.DMA((ctx_count * units,)),
        ],
        compiler_params=pltpu.CompilerParams(
            collective_id=0, has_side_effects=True, vmem_limit_bytes=60 * 1024 * 1024
        ),
    )(block_picks, lengths, jnp.swapaxes(queries, 1, 2), latent_cache.T)


def solution(mesh):
    placed = (
        P(("groups", "ctx"), None, None),
        P(("groups", "ctx"), None),
        P(("groups", "ctx"), None),
        P(("groups", "ctx")),
    )
    return jax.shard_map(
        shards,
        mesh=mesh,
        in_specs=placed,
        out_specs=P(("groups", "ctx"), None, None),
        check_vma=False,
    )
```

profile of v0, /device:TPU:0, one launch (start us, length us, event | category | flops | bytes accessed | tf_op | source)
XLA Modules:
  0.0 81.8 jit_solution(2605058320554150366)
XLA Ops:
  0.0 78.7 %shard_map.46 = bf16[16,128,512]{2,1,0:T(8,128)(2,1)} custom-call(s32[1,32]{1,0:T(1,128)} %picks_ref.1, s32[16]{0:T(128)} %lengths_ref.1, bf16[16,576,128]{2,1,0:T(8,128)(2,1)} %bitcast.2, bf16[576,1024]{1,0:T(8,128)(2,1)} %bitcast.3), custom_call_target="tpu_custom_call" | custom-call | tf_op jit(solution)/shard_map/pallas_call | solution.py:372
  78.7 3.1 %copy.6 = bf16[16,128,512]{2,1,0:T(8,128)(2,1)} copy(bf16[16,128,512]{2,1,0:T(8,128)(2,1)} %shard_map.46) | data formatting | bytes 4194304
where the time goes:
time: 82 us; the launch traced here: 81.8 us
  Pallas kernels  78.7 us (96%)
  local copies, waits for them, and re-layouts  3.1 us (4%)
    pallas_call x1, Pallas kernels, shards(): pl.pallas_call(functools.partial(step_kernel, ctx_count, owned, units), o...  78.7 us
    unnamed x1, local copies, waits for them, and re-layouts  3.1 us

commit v1 on v0

--- a/solution.py
+++ b/solution.py
@@ -371,7 +371,7 @@
     keys = TOPK * BLOCK
     return pl.pallas_call(
         functools.partial(step_kernel, ctx_count, owned, units),
-        out_shape=jax.ShapeDtypeStruct((rows, heads, LAT), jnp.bfloat16),
+        out_shape=pltpu.VMEM((rows, heads, LAT), jnp.bfloat16),
         in_specs=[
             pl.BlockSpec(memory_space=pltpu.SMEM),
             pl.BlockSpec(memory_space=pltpu.SMEM),
@@ -402,7 +402,7 @@
             pltpu.SemaphoreType.DMA((ctx_count * units,)),
         ],
         compiler_params=pltpu.CompilerParams(
-            collective_id=0, has_side_effects=True, vmem_limit_bytes=60 * 1024 * 1024
+            collective_id=0, has_side_effects=True, vmem_limit_bytes=64_900_000
         ),
     )(block_picks, lengths, jnp.swapaxes(queries, 1, 2), latent_cache.T)
 

time: 82 us -> 78.8 us (0.961)
  local copies, waits for them, and re-layouts: 3.1 us -> 1.32 us
  Pallas kernels: 78.7 us -> 77.3 us
    unnamed x1, local copies, waits for them, and re-layouts: 3.1 us -> 1.32 us
    pallas_call x1, Pallas kernels: 78.7 us -> 77.3 us  [shards(): pl.pallas_call(functools.partial(step_kernel, ctx_count, owned, units), o...]
where the time goes in v1:
time: 78.8 us; the launch traced here: 78.7 us
  Pallas kernels  77.3 us (98%)
  local copies, waits for them, and re-layouts  1.32 us (2%)
    pallas_call x1, Pallas kernels, shards(): pl.pallas_call(functools.partial(step_kernel, ctx_count, owned, units), o...  77.3 us

profile of v1, /device:TPU:0, one launch (start us, length us, event | category | flops | bytes accessed | tf_op | source)
XLA Modules:
  0.0 78.7 jit_solution(6532893510475038943)
XLA Ops:
  0.0 77.3 %shard_map.46 = bf16[16,128,512]{2,1,0:T(8,128)(2,1)S(1)} custom-call(s32[1,32]{1,0:T(1,128)} %picks_ref.1, s32[16]{0:T(128)} %lengths_ref.1, bf16[16,576,128]{2,1,0:T(8,128)(2,1)} %bitcast.2, bf16[576,1024]{1,0:T(8,128)(2,1)} %bitcast.3), custom_call_target="tpu_custom_call" | custom-call | tf_op jit(solution)/shard_map/pallas_call | solution.py:372
  77.4 1.3 %copy.6 = bf16[16,128,512]{2,1,0:T(8,128)(2,1)} copy(bf16[16,128,512]{2,1,0:T(8,128)(2,1)S(1)} %shard_map.46) | data formatting | bytes 4194304

commit v2 on v1

v2 whole, which is shorter than its diff:
```python
import functools

import jax
import jax.numpy as jnp
from jax import lax
from jax.experimental import pallas as pl
from jax.experimental.pallas import tpu as pltpu
from jax.sharding import PartitionSpec as P

LAT = 512
BLOCK = 64
TOPK = 32
LANES = 128

SOFTMAX_SCALE = 192.0 ** (-0.5)
LOG2E = 1.4426950408889634
MESH = pl.DeviceIdType.MESH
HIDDEN = -1e30
CHUNK = 4


def step_kernel(
    ctx_count, owned, units, picks_ref, lengths_ref, queries_ref, cache_ref, out_ref,
    raw_q, near_cache, q_ref, flags_ref, all_flags, gath, pool, tails, keys, positions, order, slots,
    top_ref, total_ref, acc_ref, s_a, s_b, p_a, p_b, h_a, h_b,
    q_sem, cache_sem, flag_send, flag_recv, send, recv,
):
    rows, feature, heads = queries_ref.shape
    rope = feature - LAT
    pair = 2 * BLOCK
    tall = pair * rope // LAT
    line = ctx_count // 4
    span = max(1, units // 2)
    crossing = span if units > 1 else 0
    me = lax.axis_index("ctx")
    core = lax.rem(me, 2)
    y = lax.rem(me // 2, 2)
    z = me // 4

    fetch = pltpu.make_async_copy(queries_ref, raw_q, q_sem)
    fetch_cache = pltpu.make_async_copy(cache_ref, near_cache, cache_sem)
    fetch_cache.start()
    fetch.start()

    def at(zz, yy, cc):
        return (zz * 2 + yy) * 2 + cc

    barrier = pltpu.get_barrier_semaphore()

    @pl.loop(1, ctx_count)
    def _(d):
        pl.semaphore_signal(
            barrier, inc=1, device_id={"ctx": lax.rem(me + d, ctx_count)}, device_id_type=MESH
        )

    flag_rows = flags_ref.shape[0]
    block_id = lax.broadcasted_iota(jnp.int32, (flag_rows, LANES), 0) * LANES
    block_id += lax.broadcasted_iota(jnp.int32, (flag_rows, LANES), 1)
    lane = lax.broadcasted_iota(jnp.int32, (1, LANES), 1)
    flags = jnp.zeros((flag_rows, LANES), jnp.int32)
    for k in range(TOPK):
        flags = jnp.where(block_id == picks_ref[0, k], 1, flags)
    flags_ref[...] = flags

    pl.semaphore_wait(barrier, ctx_count - 1)

    def flag_copy(d):
        return pltpu.make_async_remote_copy(
            src_ref=flags_ref,
            dst_ref=all_flags.at[me],
            send_sem=flag_send.at[d],
            recv_sem=flag_recv.at[me],
            device_id={"ctx": lax.rem(me + d, ctx_count)},
            device_id_type=MESH,
        )

    def flag_arrival(source):
        return pltpu.make_async_remote_copy(
            src_ref=flags_ref,
            dst_ref=all_flags.at[source],
            send_sem=flag_send.at[0],
            recv_sem=flag_recv.at[source],
            device_id={"ctx": source},
            device_id_type=MESH,
        )

    @pl.loop(1, ctx_count)
    def _(d):
        flag_copy(d).start()

    all_flags[me] = flags

    def stage(p):
        owner = p // owned
        away = jnp.abs(owner // 4 - z)
        aside = (lax.rem(owner // 2, 2) != y).astype(jnp.int32)
        c = lax.rem(owner, 2)
        last = 3 + 2 * c + aside
        return jnp.where(away == line - 1, last, jnp.where(away == line - 2, aside * (1 + c), 0))

    stages = [stage(picks_ref[0, k]) for k in range(TOPK)]
    begin, total = [], jnp.int32(0)
    for v in range(7):
        begin.append(total)
        for k in range(TOPK):
            total += (stages[k] == v).astype(jnp.int32)
    ordered = jnp.zeros((1, LANES), jnp.int32)
    for k in range(TOPK):
        place = jnp.int32(0)
        for v in range(7):
            here = (stages[k] == v).astype(jnp.int32)
            place += here * begin[v]
            begin[v] += here
        ordered = jnp.where(lane == place, picks_ref[0, k], ordered)

    @pl.loop(1, ctx_count)
    def _(d):
        flag_arrival(lax.rem(me + d, ctx_count)).wait_recv()

    named = jnp.minimum(jnp.max(all_flags[...], axis=0), 1)
    mine = (named > 0) & (block_id // owned == me)

    def unit_copy(slot, local, way, target):
        return pltpu.make_async_remote_copy(
            src_ref=gath.at[slot],
            dst_ref=gath.at[slot],
            send_sem=send.at[local, way],
            recv_sem=recv.at[slot],
            device_id={"ctx": target},
            device_id_type=MESH,
        )

    def item(path, i):
        if units > 1:
            return i // span, path * span + lax.rem(i, span)
        return path, i * 0

    def slot_of(zz, j):
        crossed = (j == units).astype(jnp.int32)
        i = jnp.where(j == units, crossing, j)
        yy = lax.rem(y + crossed, 2)
        c, u = item(core, i)
        return at(zz, yy, c) * units + u, (zz * 2 + yy) * units + i, c

    up = at(lax.rem(z + 1, line), y, core)
    down = at(lax.rem(z + line - 1, line), y, core)
    across = at(z, 1 - y, core)
    sibling = at(z, y, 1 - core)

    def sends(zz, j, c):
        valid = (zz >= 0) & (zz < line) & ((j < units) | (core == 1))
        own_line = j < units
        return (
            (0, up, valid & (zz <= z) & (z + 1 < line)),
            (1, down, valid & (zz >= z) & (z > 0)),
            (2, across, valid & own_line & ((zz == z) | (core == 0) | (j != crossing))),
            (3, sibling, valid & ((zz != z) | (j == units) | (c == core))),
        )

    def forward(zz, j, skip=()):
        slot, local, c = slot_of(zz, j)
        for way, target, yes in sends(zz, j, c):
            if way not in skip:
                @pl.when(yes)
                def _():
                    unit_copy(slot, local, way, target).start()

    def arrived(slot):
        unit_copy(slot, 0, 0, sibling).wait_recv()

    def keep(slot):
        pool[2 * slot] = gath[slot, :BLOCK]
        pool[2 * slot + 1] = gath[slot, BLOCK:pair]
        tails[slot] = gath[slot, pair:]

    past = ctx_count * owned
    fetch_cache.wait()
    token = lax.broadcasted_iota(jnp.int32, (pair, owned * BLOCK), 0)
    column = lax.broadcasted_iota(jnp.int32, (pair, owned * BLOCK), 1)
    starts = []
    last = jnp.int32(-1)
    for _ in range(2 * units):
        last = jnp.min(jnp.where(mine & (block_id > last), block_id, past))
        starts.append(jnp.minimum(last - me * owned, owned - 1) * BLOCK)

    def other_path(u):
        return (z * 2 + y) * units + (1 - core) * span + u % span

    for u in [v for r in range(span) for v in range(r, units, span)]:
        first, second = starts[2 * u], starts[2 * u + 1]
        wanted = jnp.where(token < BLOCK, first + token, second + token - BLOCK)
        chosen = jnp.where(column == wanted, 1.0, 0.0).astype(jnp.bfloat16)
        tokens = lax.dot_general(
            chosen, near_cache[...], (((1,), (1,)), ((), ())), preferred_element_type=jnp.float32
        ).astype(jnp.bfloat16)
        tail = tokens[:, LAT:]
        packed = jnp.concatenate(
            [tail[i * tall : (i + 1) * tall, :] for i in range(pair // tall)], axis=1
        )
        gath[me * units + u, :pair, :] = tokens[:, :LAT]
        gath[me * units + u, pair:, :] = packed
        pool[2 * (me * units + u)] = tokens[:BLOCK, :LAT]
        pool[2 * (me * units + u) + 1] = tokens[BLOCK:, :LAT]
        tails[me * units + u] = packed
        if units == 1:
            forward(z, jnp.int32(0))
        else:
            path = u // span
            position = jnp.int32(path * span + u % span)

            @pl.when((core == path) & (core == 0))
            def _():
                forward(z, position)

            @pl.when((core == path) & (core == 1))
            def _():
                forward(z, position, (0, 1, 2))

            @pl.when(core != path)
            def _():
                unit_copy(me * units + u, other_path(u), 3, sibling).start()

    if units > 1:
        @pl.loop(0, units)
        def _(i):
            slot, _, c = slot_of(z, i)

            @pl.when(c != core)
            def _():
                arrived(slot)
                forward(z, i)
                keep(slot)

            @pl.when((c == core) & (core == 1))
            def _():
                forward(z, i, (3,))

    fetch.wait()

    for k in range(TOPK):
        p = jnp.sum(jnp.where(lane == k, ordered, 0))
        order[k] = p
        below = (block_id // owned == p // owned) & (block_id < p)
        slots[k] = jnp.sum(jnp.where(below, named, 0))

    def sides(d):
        return ((z + d, d >= 0), (z - d, d > 0))

    def along(d, j):
        for zz, yes in sides(d):
            @pl.when(yes & (zz >= 0) & (zz < line) & ((j < units) | (core == 1)))
            def _():
                slot, _, _ = slot_of(zz, j)
                arrived(slot)
                forward(zz, j)
                keep(slot)

    def cross(d, i):
        for zz, yes in sides(d):
            @pl.when(yes & (zz >= 0) & (zz < line) & ((core == 0) | (i != crossing)))
            def _():
                c, u = item(core, i)
                slot = at(zz, 1 - y, c) * units + u
                arrived(slot)
                unit_copy(slot, (zz * 2 + 1 - y) * units + i, 3, sibling).start()
                keep(slot)

    def beside(d, aside, i):
        c, u = item(1 - core, i)
        for zz, yes in sides(d):
            there = yes & (zz >= 0) & (zz < line)
            if not aside:
                there &= (d > 0) | (c != core)

            @pl.when(there)
            def _():
                yy = 1 - y if aside else y
                slot = at(zz, yy, c) * units + u
                arrived(slot)
                keep(slot)

    def each(c, path, body, lo=0, hi=None):
        if units > 1:
            pl.loop(c * span + lo, c * span + (span if hi is None else hi))(body)
        elif lo == 0:
            pl.when(path == c)(lambda: body(jnp.int32(0)))

    def cross_owner(d, c, lo=0, hi=None):
        each(c, core, lambda i: cross(jnp.int32(d), i), lo, hi)

    def along_owner(d, c, lo=0, hi=None):
        each(c, core, lambda i: along(jnp.int32(d), i), lo, hi)

    def beside_owner(d, aside, c):
        each(c, 1 - core, lambda i: beside(jnp.int32(d), aside, i))

    per = units + 1
    main = per * (line - 2)
    share = -(-rows // main)

    @pl.loop(0, main)
    def _(k):
        d = k // per + 1
        j = lax.rem(k, per)
        along(d, j)

        @pl.when((k == span) & (core == 1))
        def _():
            slot, _, _ = slot_of(z, jnp.int32(units))
            arrived(slot)
            forward(z, jnp.int32(units))
            keep(slot)

        @pl.when(j < units)
        def _():
            cross(d - 1, j)
            beside(d - 1, False, j)

        @pl.when((j < units) & (d > 1))
        def _():
            beside(d - 2, True, j)

        for r in range(share):
            @pl.when(k * share + r < rows)
            def _():
                row = lax.rem(k * share + r, rows)
                q_ref[row] = raw_q[row].T
                total_ref[pl.ds(row * heads, heads)] = jnp.zeros((heads, 1), jnp.float32)
                top_ref[pl.ds(row * heads, heads)] = jnp.full((heads, 1), HIDDEN, jnp.float32)
                acc_ref[pl.ds(row * heads, heads)] = jnp.zeros((heads, LAT), jnp.float32)

    @pl.loop(0, units)
    def _(i):
        beside(jnp.int32(line - 2), False, i)
        beside(jnp.int32(line - 3), True, i)

    scale = SOFTMAX_SCALE * LOG2E
    deep = CHUNK * BLOCK
    rowset = 4 if rows % 4 == 0 else 1
    groups = rows // rowset
    height = rowset * heads
    parts = 2 if rowset % 2 == 0 else 1

    def fill(n):
        places = []
        for k in range(CHUNK):
            p, slot = order[n * CHUNK + k], slots[n * CHUNK + k]
            here = slice(k * BLOCK, (k + 1) * BLOCK)
            keys[here, :LAT] = pool[p // owned * (2 * units) + slot]
            both = tails[p // owned * units + slot // 2]
            tail = jnp.where(lax.rem(slot, 2) == 0, both[:, : LAT // 2], both[:, LAT // 2 :])
            keys[here, LAT:] = jnp.concatenate(
                [tail[:, i * rope : (i + 1) * rope] for i in range(BLOCK // tall)], axis=0
            )
            places.append(p * BLOCK)
        for k in range(0, CHUNK, 2):
            positions[:, k * BLOCK : (k + 2) * BLOCK] = jnp.where(
                lane < BLOCK, places[k] + lane, places[k + 1] + lane - BLOCK
            )

    def qk(g, s_ref):
        for t in range(parts):
            low, many = g * rowset + t * rowset // parts, rowset // parts
            s_ref[t * height // parts : (t + 1) * height // parts] = lax.dot_general(
                q_ref[low : low + many].reshape(many * heads, feature), keys[...],
                (((1,), (1,)), ((), ())), preferred_element_type=jnp.float32,
            )

    def soft(g, s_ref, p_ref, h_ref):
        span_g = slice(g * height, (g + 1) * height)
        where = positions[...]
        s = jnp.concatenate(
            [
                jnp.where(
                    where < lengths_ref[g * rowset + r], s_ref[r * heads : (r + 1) * heads], HIDDEN
                )
                for r in range(rowset)
            ],
            axis=0,
        )
        before = top_ref[span_g]
        top = jnp.maximum(before, jnp.max(s, axis=1, keepdims=True))
        e = jnp.exp2((s - top) * scale)
        shrink = jnp.exp2((before - top) * scale)
        total_ref[span_g] = total_ref[span_g] * shrink + jnp.sum(e, axis=1, keepdims=True)
        top_ref[span_g] = top
        p_ref[...] = e.astype(jnp.bfloat16)
        h_ref[...] = shrink

    def pv(g, p_ref, h_ref, final):
        span_g = slice(g * height, (g + 1) * height)
        o = acc_ref[span_g] * h_ref[...] + jnp.dot(
            p_ref[...], keys[:, :LAT], preferred_element_type=jnp.float32
        )
        if final:
            o = (o / total_ref[span_g]).astype(jnp.bfloat16)
            out_ref[g * rowset : (g + 1) * rowset] = o.reshape(rowset, heads, LAT)
        else:
            acc_ref[span_g] = o

    def attend(n, final=False):
        fill(n)
        s, p, h = (s_a, s_b), (p_a, p_b), (h_a, h_b)
        for g in range(groups + 2):
            if g < groups:
                qk(g, s[g % 2])
            if 1 <= g <= groups:
                soft(g - 1, s[(g - 1) % 2], p[(g - 1) % 2], h[(g - 1) % 2])
            if g >= 2:
                pv(g - 2, p[g % 2], h[g % 2], final)

    ready = [(TOPK - (6 - v) * units) // CHUNK for v in range(7)]

    def attend_ready(v, lo=None, hi=None):
        lo = (ready[v - 1] if v else 0) if lo is None else lo
        hi = min(ready[v], TOPK // CHUNK - 1) if hi is None else hi
        if hi - lo == 1:
            attend(lo)
        elif hi > lo:
            pl.loop(lo, hi)(lambda n: attend(n))

    attend_ready(0, hi=1)
    cross_owner(line - 2, 0)
    attend_ready(0, lo=1)
    along_owner(line - 1, 0, 0, 1)
    beside_owner(line - 2, True, 0)
    attend_ready(1)
    cross_owner(line - 2, 1)
    along_owner(line - 1, 0, 1)
    beside_owner(line - 2, True, 1)
    attend_ready(2)
    along_owner(line - 1, 1, 0, 1)
    cross_owner(line - 1, 0, 0, 1)
    beside_owner(line - 1, False, 0)
    attend_ready(3)
    cross_owner(line - 1, 0, 1)
    along_owner(line - 1, 1, 1)
    beside_owner(line - 1, True, 0)
    attend_ready(4)
    along(jnp.int32(line - 1), jnp.int32(units))
    cross_owner(line - 1, 1, 0, 1)
    beside_owner(line - 1, False, 1)
    attend_ready(5)
    cross_owner(line - 1, 1, 1)
    beside_owner(line - 1, True, 1)
    attend(TOPK // CHUNK - 1, final=True)

    @pl.loop(1, ctx_count)
    def _(d):
        flag_copy(d).wait_send()

    @pl.loop(0, per * line)
    def _(k):
        zz = k // per
        j = lax.rem(k, per)
        slot, local, c = slot_of(zz, j)
        for way, target, yes in sends(zz, j, c):
            @pl.when(yes)
            def _():
                unit_copy(slot, local, way, target).wait_send()

    @pl.loop(0, units * line)
    def _(k):
        zz = k // units
        i = lax.rem(k, units)

        @pl.when((core == 0) | (i != crossing))
        def _():
            c, u = item(core, i)
            slot = at(zz, 1 - y, c) * units + u
            unit_copy(slot, (zz * 2 + 1 - y) * units + i, 3, sibling).wait_send()

    if units > 1:
        for u in range(units):
            @pl.when(core != u // span)
            def _():
                unit_copy(me * units + u, other_path(u), 3, sibling).wait_send()


def shards(queries, latent_cache, block_picks, lengths):
    ctx_count = lax.axis_size("ctx")
    rows, heads, feature = queries.shape
    owned = latent_cache.shape[0] // BLOCK
    units = max(1, 2 * TOPK // ctx_count)
    flag_rows = -(-(ctx_count * owned) // LANES // 8) * 8
    tall = 2 * BLOCK + 2 * BLOCK * (feature - LAT) // LAT
    height = (4 if rows % 4 == 0 else 1) * heads
    return pl.pallas_call(
        functools.partial(step_kernel, ctx_count, owned, units),
        out_shape=pltpu.VMEM((rows, heads, LAT), jnp.bfloat16),
        in_specs=[
            pl.BlockSpec(memory_space=pltpu.SMEM),
            pl.BlockSpec(memory_space=pltpu.SMEM),
            pl.BlockSpec(memory_space=pl.ANY),
            pl.BlockSpec(memory_space=pl.ANY),
        ],
        out_specs=pl.BlockSpec(memory_space=pltpu.VMEM),
        scratch_shapes=[
            pltpu.VMEM((rows, feature, heads), jnp.bfloat16),
            pltpu.VMEM((feature, owned * BLOCK), jnp.bfloat16),
            pltpu.VMEM((rows, heads, feature), jnp.bfloat16),
            pltpu.VMEM((flag_rows, LANES), jnp.int32),
            pltpu.VMEM((ctx_count, flag_rows, LANES), jnp.int32),
            pltpu.VMEM((ctx_count * units, tall, LAT), jnp.bfloat16),
            pltpu.VMEM((ctx_count * units * 2, BLOCK, LAT), jnp.bfloat16),
            pltpu.VMEM((ctx_count * units, tall - 2 * BLOCK, LAT), jnp.bfloat16),
            pltpu.VMEM((CHUNK * BLOCK, feature), jnp.bfloat16),
            pltpu.VMEM((1, CHUNK * BLOCK), jnp.int32),
            pltpu.SMEM((TOPK,), jnp.int32),
            pltpu.SMEM((TOPK,), jnp.int32),
            pltpu.VMEM((rows * heads, 1), jnp.float32),
            pltpu.VMEM((rows * heads, 1), jnp.float32),
            pltpu.VMEM((rows * heads, LAT), jnp.float32),
            *[pltpu.VMEM((height, CHUNK * BLOCK), jnp.float32)] * 2,
            *[pltpu.VMEM((height, CHUNK * BLOCK), jnp.bfloat16)] * 2,
            *[pltpu.VMEM((height, 1), jnp.float32)] * 2,
            pltpu.SemaphoreType.DMA,
            pltpu.SemaphoreType.DMA,
            pltpu.SemaphoreType.DMA((ctx_count,)),
            pltpu.SemaphoreType.DMA((ctx_count,)),
            pltpu.SemaphoreType.DMA((ctx_count // 2 * units, 4)),
            pltpu.SemaphoreType.DMA((ctx_count * units,)),
        ],
        compiler_params=pltpu.CompilerParams(
            collective_id=0, has_side_effects=True, vmem_limit_bytes=64_900_000
        ),
    )(block_picks, lengths, jnp.swapaxes(queries, 1, 2), latent_cache.T)


def solution(mesh):
    placed = (
        P(("groups", "ctx"), None, None),
        P(("groups", "ctx"), None),
        P(("groups", "ctx"), None),
        P(("groups", "ctx")),
    )
    return jax.shard_map(
        shards,
        mesh=mesh,
        in_specs=placed,
        out_specs=P(("groups", "ctx"), None, None),
        check_vma=False,
    )
```

time: 78.8 us -> 75.2 us (0.954)
  the two profiles are of different devices: /device:TPU:0 before, /device:TPU:19 now
where the time goes in v2:
time: 75.2 us; the launch traced here: 75.1 us
  Pallas kernels  73.8 us (98%)
  local copies, waits for them, and re-layouts  1.32 us (2%)
    pallas_call x1, Pallas kernels, shards(): pl.pallas_call(functools.partial(step_kernel, ctx_count, owned, units), o...  73.8 us

profile of v2, /device:TPU:19, one launch (start us, length us, event | category | flops | bytes accessed | tf_op | source)
XLA Modules:
  0.0 75.1 jit_solution(16435353836460827777)
XLA Ops:
  0.0 73.8 %shard_map.46 = bf16[16,128,512]{2,1,0:T(8,128)(2,1)S(1)} custom-call(s32[1,32]{1,0:T(1,128)} %picks_ref.1, s32[16]{0:T(128)} %lengths_ref.1, bf16[16,576,128]{2,1,0:T(8,128)(2,1)} %bitcast.2, bf16[576,1024]{1,0:T(8,128)(2,1)} %bitcast.3), custom_call_target="tpu_custom_call" | custom-call | tf_op jit(solution)/shard_map/pallas_call | solution.py:488
  73.8 1.3 %copy.6 = bf16[16,128,512]{2,1,0:T(8,128)(2,1)} copy(bf16[16,128,512]{2,1,0:T(8,128)(2,1)S(1)} %shard_map.46) | data formatting | bytes 4194304

commit v3 on v2

--- a/solution.py
+++ b/solution.py
@@ -18,12 +18,26 @@
 HIDDEN = -1e30
 CHUNK = 4
 
+EDGE = (
+    110, 500, 111, 201, 113, 600, 202, 211, 301, 302, 114, 112, 300, 401, 311, 600, 120, 310,
+    121, 212, 210, 313, 203, 321, 213, 600, 122, 320, 410, 402, 411, 200, 412, 220, 303, 312,
+    123, 400, 413, 600, 403, 700, 221, 232, 420, 130, 124, 222, 323, 322, 701, 223, 422, 421,
+    131, 702, 331, 330, 132, 423, 230, 703, 332, 133, 231, 704, 431, 430, 333, 705, 134, 233,
+    706, 432, 433, 707,
+)
+INNER = (
+    600, 500, 301, 202, 112, 110, 111, 600, 114, 402, 210, 410, 212, 312, 303, 310, 203, 200,
+    113, 600, 311, 313, 120, 400, 403, 302, 600, 201, 211, 121, 321, 401, 122, 300, 123, 320,
+    700, 323, 124, 322, 213, 701, 413, 222, 411, 702, 412, 422, 703, 704, 220, 223, 221, 705,
+    420, 421, 423, 706, 707,
+)
+
 
 def step_kernel(
     ctx_count, owned, units, picks_ref, lengths_ref, queries_ref, cache_ref, out_ref,
-    raw_q, near_cache, q_ref, flags_ref, all_flags, gath, pool, tails, keys, positions, order, slots,
+    raw_q, near_cache, q_ref, flags_ref, all_flags, gath, pool, tails, keys, positions, listed_v, listed,
     top_ref, total_ref, acc_ref, s_a, s_b, p_a, p_b, h_a, h_b,
-    q_sem, cache_sem, flag_send, flag_recv, send, recv,
+    q_sem, cache_sem, list_sem, flag_send, flag_recv, send, recv,
 ):
     rows, feature, heads = queries_ref.shape
     rope = feature - LAT
@@ -90,24 +104,32 @@
 
     all_flags[me] = flags
 
+    scripted = line == 4 and units == 4 and TOPK // CHUNK == 8
+    edge = (z == 0) | (z == line - 1)
+
     def stage(p):
         owner = p // owned
         away = jnp.abs(owner // 4 - z)
         aside = (lax.rem(owner // 2, 2) != y).astype(jnp.int32)
         c = lax.rem(owner, 2)
+        if scripted:
+            near = jnp.where(aside == 1, 2 + c, c)
+            outer = jnp.where(away == 3, 4 + 2 * c + aside, jnp.where(away == 2, near, 0))
+            near = jnp.where(away == 1, aside * (2 + 2 * c), 0)
+            return jnp.where(edge, outer, jnp.where(away == 2, aside * 6 + c, near))
         last = 3 + 2 * c + aside
         return jnp.where(away == line - 1, last, jnp.where(away == line - 2, aside * (1 + c), 0))
 
     stages = [stage(picks_ref[0, k]) for k in range(TOPK)]
     begin, total = [], jnp.int32(0)
-    for v in range(7):
+    for v in range(8):
         begin.append(total)
         for k in range(TOPK):
             total += (stages[k] == v).astype(jnp.int32)
     ordered = jnp.zeros((1, LANES), jnp.int32)
     for k in range(TOPK):
         place = jnp.int32(0)
-        for v in range(7):
+        for v in range(8):
             here = (stages[k] == v).astype(jnp.int32)
             place += here * begin[v]
             begin[v] += here
@@ -135,6 +157,14 @@
             return i // span, path * span + lax.rem(i, span)
         return path, i * 0
 
+    def detoured(zz):
+        if units > 1:
+            return (core == 1) | (zz == 0) | (zz == line - 1)
+        return core == 1
+
+    def plain(zz, i):
+        return jnp.logical_not(detoured(zz)) | (i != crossing)
+
     def slot_of(zz, j):
         crossed = (j == units).astype(jnp.int32)
         i = jnp.where(j == units, crossing, j)
@@ -148,12 +178,12 @@
     sibling = at(z, y, 1 - core)
 
     def sends(zz, j, c):
-        valid = (zz >= 0) & (zz < line) & ((j < units) | (core == 1))
+        valid = (zz >= 0) & (zz < line) & ((j < units) | detoured(zz))
         own_line = j < units
         return (
             (0, up, valid & (zz <= z) & (z + 1 < line)),
             (1, down, valid & (zz >= z) & (z > 0)),
-            (2, across, valid & own_line & ((zz == z) | (core == 0) | (j != crossing))),
+            (2, across, valid & own_line & ((zz == z) | plain(zz, j))),
             (3, sibling, valid & ((zz != z) | (j == units) | (c == core))),
         )
 
@@ -179,14 +209,14 @@
     column = lax.broadcasted_iota(jnp.int32, (pair, owned * BLOCK), 1)
     starts = []
     last = jnp.int32(-1)
-    for _ in range(2 * units):
-        last = jnp.min(jnp.where(mine & (block_id > last), block_id, past))
-        starts.append(jnp.minimum(last - me * owned, owned - 1) * BLOCK)
 
     def other_path(u):
         return (z * 2 + y) * units + (1 - core) * span + u % span
 
     for u in [v for r in range(span) for v in range(r, units, span)]:
+        while len(starts) < 2 * u + 2:
+            last = jnp.min(jnp.where(mine & (block_id > last), block_id, past))
+            starts.append(jnp.minimum(last - me * owned, owned - 1) * BLOCK)
         first, second = starts[2 * u], starts[2 * u + 1]
         wanted = jnp.where(token < BLOCK, first + token, second + token - BLOCK)
         chosen = jnp.where(column == wanted, 1.0, 0.0).astype(jnp.bfloat16)
@@ -237,27 +267,43 @@
 
     fetch.wait()
 
-    for k in range(TOPK):
-        p = jnp.sum(jnp.where(lane == k, ordered, 0))
-        order[k] = p
-        below = (block_id // owned == p // owned) & (block_id < p)
-        slots[k] = jnp.sum(jnp.where(below, named, 0))
-
-    def sides(d):
-        return ((z + d, d >= 0), (z - d, d > 0))
-
-    def along(d, j):
-        for zz, yes in sides(d):
-            @pl.when(yes & (zz >= 0) & (zz < line) & ((j < units) | (core == 1)))
+    within = lax.rem(block_id, owned)
+    before = named
+    shift = 1
+    while shift < owned:
+        before += jnp.where(within >= shift, pltpu.roll(before, shift, 1), 0)
+        shift *= 2
+    before -= named
+    wide = lax.broadcasted_iota(jnp.int32, (TOPK, LANES), 1)
+    tall_id = lax.broadcasted_iota(jnp.int32, (TOPK, LANES), 0)
+    column_p = jnp.sum(jnp.where(wide == tall_id, ordered, 0), axis=1, keepdims=True)
+    found = jnp.zeros((TOPK, LANES), jnp.int32)
+    for r in range(-(-past // LANES)):
+        found += jnp.where(column_p == wide + r * LANES, before[r : r + 1, :], 0)
+    column_s = jnp.sum(found, axis=1, keepdims=True)
+    listed_v[...] = jnp.where(wide == 0, column_p, column_s)
+    listing = pltpu.make_async_copy(listed_v, listed, list_sem)
+    listing.start()
+
+    def sides(d, inner=True):
+        if not scripted:
+            return ((z + d, d >= 0), (z - d, d > 0))
+        if inner and d == 1:
+            return ((z + 1, True), (z - 1, True))
+        return ((jnp.where(z + d < line, z + d, z - d), True),)
+
+    def along(d, j, inner=True):
+        for zz, yes in sides(d, inner):
+            @pl.when(yes & (zz >= 0) & (zz < line) & ((j < units) | detoured(zz)))
             def _():
                 slot, _, _ = slot_of(zz, j)
                 arrived(slot)
                 forward(zz, j)
                 keep(slot)
 
-    def cross(d, i):
-        for zz, yes in sides(d):
-            @pl.when(yes & (zz >= 0) & (zz < line) & ((core == 0) | (i != crossing)))
+    def cross(d, i, inner=True):
+        for zz, yes in sides(d, inner):
+            @pl.when(yes & (zz >= 0) & (zz < line) & plain(zz, i))
             def _():
                 c, u = item(core, i)
                 slot = at(zz, 1 - y, c) * units + u
@@ -265,9 +311,9 @@
                 unit_copy(slot, (zz * 2 + 1 - y) * units + i, 3, sibling).start()
                 keep(slot)
 
-    def beside(d, aside, i):
+    def beside(d, aside, i, inner=True):
         c, u = item(1 - core, i)
-        for zz, yes in sides(d):
+        for zz, yes in sides(d, inner):
             there = yes & (zz >= 0) & (zz < line)
             if not aside:
                 there &= (d > 0) | (c != core)
@@ -295,44 +341,20 @@
         each(c, 1 - core, lambda i: beside(jnp.int32(d), aside, i))
 
     per = units + 1
-    main = per * (line - 2)
-    share = -(-rows // main)
-
-    @pl.loop(0, main)
-    def _(k):
-        d = k // per + 1
-        j = lax.rem(k, per)
-        along(d, j)
-
-        @pl.when((k == span) & (core == 1))
+
+    def crossing_unit():
+        @pl.when(detoured(z))
         def _():
             slot, _, _ = slot_of(z, jnp.int32(units))
             arrived(slot)
             forward(z, jnp.int32(units))
             keep(slot)
 
-        @pl.when(j < units)
-        def _():
-            cross(d - 1, j)
-            beside(d - 1, False, j)
-
-        @pl.when((j < units) & (d > 1))
-        def _():
-            beside(d - 2, True, j)
-
-        for r in range(share):
-            @pl.when(k * share + r < rows)
-            def _():
-                row = lax.rem(k * share + r, rows)
-                q_ref[row] = raw_q[row].T
-                total_ref[pl.ds(row * heads, heads)] = jnp.zeros((heads, 1), jnp.float32)
-                top_ref[pl.ds(row * heads, heads)] = jnp.full((heads, 1), HIDDEN, jnp.float32)
-                acc_ref[pl.ds(row * heads, heads)] = jnp.zeros((heads, LAT), jnp.float32)
-
-    @pl.loop(0, units)
-    def _(i):
-        beside(jnp.int32(line - 2), False, i)
-        beside(jnp.int32(line - 3), True, i)
+    def prepare(row):
+        q_ref[row] = raw_q[row].T
+        total_ref[pl.ds(row * heads, heads)] = jnp.zeros((heads, 1), jnp.float32)
+        top_ref[pl.ds(row * heads, heads)] = jnp.full((heads, 1), HIDDEN, jnp.float32)
+        acc_ref[pl.ds(row * heads, heads)] = jnp.zeros((heads, LAT), jnp.float32)
 
     scale = SOFTMAX_SCALE * LOG2E
     deep = CHUNK * BLOCK
@@ -344,7 +366,7 @@
     def fill(n):
         places = []
         for k in range(CHUNK):
-            p, slot = order[n * CHUNK + k], slots[n * CHUNK + k]
+            p, slot = listed[n * CHUNK + k, 0], listed[n * CHUNK + k, 1]
             here = slice(k * BLOCK, (k + 1) * BLOCK)
             keys[here, :LAT] = pool[p // owned * (2 * units) + slot]
             both = tails[p // owned * units + slot // 2]
@@ -393,7 +415,7 @@
             p_ref[...], keys[:, :LAT], preferred_element_type=jnp.float32
         )
         if final:
-            o = (o / total_ref[span_g]).astype(jnp.bfloat16)
+            o = (o * (1.0 / total_ref[span_g])).astype(jnp.bfloat16)
             out_ref[g * rowset : (g + 1) * rowset] = o.reshape(rowset, heads, LAT)
         else:
             acc_ref[span_g] = o
@@ -409,41 +431,113 @@
             if g >= 2:
                 pv(g - 2, p[g % 2], h[g % 2], final)
 
-    ready = [(TOPK - (6 - v) * units) // CHUNK for v in range(7)]
-
-    def attend_ready(v, lo=None, hi=None):
-        lo = (ready[v - 1] if v else 0) if lo is None else lo
-        hi = min(ready[v], TOPK // CHUNK - 1) if hi is None else hi
-        if hi - lo == 1:
-            attend(lo)
-        elif hi > lo:
-            pl.loop(lo, hi)(lambda n: attend(n))
-
-    attend_ready(0, hi=1)
-    cross_owner(line - 2, 0)
-    attend_ready(0, lo=1)
-    along_owner(line - 1, 0, 0, 1)
-    beside_owner(line - 2, True, 0)
-    attend_ready(1)
-    cross_owner(line - 2, 1)
-    along_owner(line - 1, 0, 1)
-    beside_owner(line - 2, True, 1)
-    attend_ready(2)
-    along_owner(line - 1, 1, 0, 1)
-    cross_owner(line - 1, 0, 0, 1)
-    beside_owner(line - 1, False, 0)
-    attend_ready(3)
-    cross_owner(line - 1, 0, 1)
-    along_owner(line - 1, 1, 1)
-    beside_owner(line - 1, True, 0)
-    attend_ready(4)
-    along(jnp.int32(line - 1), jnp.int32(units))
-    cross_owner(line - 1, 1, 0, 1)
-    beside_owner(line - 1, False, 1)
-    attend_ready(5)
-    cross_owner(line - 1, 1, 1)
-    beside_owner(line - 1, True, 1)
-    attend(TOPK // CHUNK - 1, final=True)
+    def generic():
+        main = per * (line - 2)
+        share = -(-rows // main)
+
+        @pl.loop(0, main)
+        def _(k):
+            d = k // per + 1
+            j = lax.rem(k, per)
+            along(d, j)
+
+            pl.when(k == span)(crossing_unit)
+
+            @pl.when(j < units)
+            def _():
+                cross(d - 1, j)
+                beside(d - 1, False, j)
+
+            @pl.when((j < units) & (d > 1))
+            def _():
+                beside(d - 2, True, j)
+
+            for r in range(share):
+                @pl.when(k * share + r < rows)
+                def _():
+                    prepare(lax.rem(k * share + r, rows))
+
+        @pl.loop(0, units)
+        def _(i):
+            beside(jnp.int32(line - 2), False, i)
+            beside(jnp.int32(line - 3), True, i)
+
+        ready = [(TOPK - (6 - v) * units) // CHUNK for v in range(7)]
+
+        def attend_ready(v, lo=None, hi=None):
+            lo = (ready[v - 1] if v else 0) if lo is None else lo
+            hi = min(ready[v], TOPK // CHUNK - 1) if hi is None else hi
+            if hi - lo == 1:
+                attend(lo)
+            elif hi > lo:
+                pl.loop(lo, hi)(lambda n: attend(n))
+
+        attend_ready(0, hi=1)
+        cross_owner(line - 2, 0)
+        attend_ready(0, lo=1)
+        along_owner(line - 1, 0, 0, 1)
+        beside_owner(line - 2, True, 0)
+        attend_ready(1)
+        cross_owner(line - 2, 1)
+        along_owner(line - 1, 0, 1)
+        beside_owner(line - 2, True, 1)
+        attend_ready(2)
+        along_owner(line - 1, 1, 0, 1)
+        cross_owner(line - 1, 0, 0, 1)
+        beside_owner(line - 1, False, 0)
+        attend_ready(3)
+        cross_owner(line - 1, 0, 1)
+        along_owner(line - 1, 1, 1)
+        beside_owner(line - 1, True, 0)
+        attend_ready(4)
+        along(jnp.int32(line - 1), jnp.int32(units))
+        cross_owner(line - 1, 1, 0, 1)
+        beside_owner(line - 1, False, 1)
+        attend_ready(5)
+        cross_owner(line - 1, 1, 1)
+        beside_owner(line - 1, True, 1)
+        attend(TOPK // CHUNK - 1, final=True)
+
+    def perform(work, inner):
+        for w in work:
+            kind, d, i = w // 100, w // 10 % 10, jnp.int32(w % 10)
+            if kind == 1:
+                along(d, i, inner)
+            elif kind == 2:
+                cross(d, i, inner)
+            elif kind in (3, 4):
+                beside(d, kind == 4, i, inner)
+            elif kind == 5:
+                crossing_unit()
+
+    def preparation(work, before):
+        shares = EDGE.count(600)
+        pl.loop(before * rows // shares, (before + work) * rows // shares)(prepare)
+
+    def pieces(work, chunk):
+        starts = [0] + [work.index(700 + n) + 1 for n in range(8)]
+        return work[starts[chunk] : starts[chunk + 1] - 1]
+
+    def emit(work, inner):
+        done, batch = 0, []
+        for w in work + (0,):
+            if w in (0, 600):
+                perform(batch, inner)
+                batch = []
+                if w:
+                    preparation(1, done)
+                    done += 1
+            else:
+                batch.append(w)
+
+    listing.wait()
+    if scripted:
+        for n in range(8):
+            pl.when(edge)(lambda: emit(pieces(EDGE, n), False))
+            pl.when(jnp.logical_not(edge))(lambda: emit(pieces(INNER, n), True))
+            attend(n, final=n == 7)
+    else:
+        generic()
 
     @pl.loop(1, ctx_count)
     def _(d):
@@ -464,7 +558,7 @@
         zz = k // units
         i = lax.rem(k, units)
 
-        @pl.when((core == 0) | (i != crossing))
+        @pl.when(plain(zz, i))
         def _():
             c, u = item(core, i)
             slot = at(zz, 1 - y, c) * units + u
@@ -506,14 +600,15 @@
             pltpu.VMEM((ctx_count * units, tall - 2 * BLOCK, LAT), jnp.bfloat16),
             pltpu.VMEM((CHUNK * BLOCK, feature), jnp.bfloat16),
             pltpu.VMEM((1, CHUNK * BLOCK), jnp.int32),
-            pltpu.SMEM((TOPK,), jnp.int32),
-            pltpu.SMEM((TOPK,), jnp.int32),
+            pltpu.VMEM((TOPK, LANES), jnp.int32),
+            pltpu.SMEM((TOPK, LANES), jnp.int32),
             pltpu.VMEM((rows * heads, 1), jnp.float32),
             pltpu.VMEM((rows * heads, 1), jnp.float32),
             pltpu.VMEM((rows * heads, LAT), jnp.float32),
             *[pltpu.VMEM((height, CHUNK * BLOCK), jnp.float32)] * 2,
             *[pltpu.VMEM((height, CHUNK * BLOCK), jnp.bfloat16)] * 2,
             *[pltpu.VMEM((height, 1), jnp.float32)] * 2,
+            pltpu.SemaphoreType.DMA,
             pltpu.SemaphoreType.DMA,
             pltpu.SemaphoreType.DMA,
             pltpu.SemaphoreType.DMA((ctx_count,)),

time: 75.2 us -> 68.5 us (0.911)
  the two profiles are of different devices: /device:TPU:19 before, /device:TPU:0 now
where the time goes in v3:
time: 68.5 us; the launch traced here: 68.1 us
  Pallas kernels  66.8 us (98%)
  local copies, waits for them, and re-layouts  1.32 us (2%)
    pallas_call x1, Pallas kernels, shards(): pl.pallas_call(functools.partial(step_kernel, ctx_count, owned, units), o...  66.8 us

profile of v3, /device:TPU:0, one launch (start us, length us, event | category | flops | bytes accessed | tf_op | source)
XLA Modules:
  0.0 68.1 jit_solution(9784578274299612486)
XLA Ops:
  0.0 66.8 %shard_map.46 = bf16[16,128,512]{2,1,0:T(8,128)(2,1)S(1)} custom-call(s32[1,32]{1,0:T(1,128)} %picks_ref.1, s32[16]{0:T(128)} %lengths_ref.1, bf16[16,576,128]{2,1,0:T(8,128)(2,1)} %bitcast.2, bf16[576,1024]{1,0:T(8,128)(2,1)} %bitcast.3), custom_call_target="tpu_custom_call" | custom-call | tf_op jit(solution)/shard_map/pallas_call | solution.py:582
  66.8 1.3 %copy.6 = bf16[16,128,512]{2,1,0:T(8,128)(2,1)} copy(bf16[16,128,512]{2,1,0:T(8,128)(2,1)S(1)} %shard_map.46) | data formatting | bytes 4194304

commit v4 on v3

--- a/solution.py
+++ b/solution.py
@@ -19,25 +19,25 @@
 CHUNK = 4
 
 EDGE = (
-    110, 500, 111, 201, 113, 600, 202, 211, 301, 302, 114, 112, 300, 401, 311, 600, 120, 310,
-    121, 212, 210, 313, 203, 321, 213, 600, 122, 320, 410, 402, 411, 200, 412, 220, 303, 312,
-    123, 400, 413, 600, 403, 700, 221, 232, 420, 130, 124, 222, 323, 322, 701, 223, 422, 421,
-    131, 702, 331, 330, 132, 423, 230, 703, 332, 133, 231, 704, 431, 430, 333, 705, 134, 233,
-    706, 432, 433, 707,
+    111, 110, 300, 500, 112, 600, 311, 113, 310, 203, 120, 320, 302, 210, 201, 122, 313, 303,
+    402, 312, 202, 211, 213, 121, 200, 411, 600, 413, 114, 403, 401, 123, 212, 600, 600, 301,
+    321, 410, 400, 412, 222, 322, 220, 700, 124, 323, 420, 130, 232, 221, 701, 223, 131, 421,
+    330, 422, 702, 423, 331, 230, 703, 133, 430, 231, 704, 132, 431, 705, 233, 333, 332, 134,
+    706, 433, 432, 707,
 )
 INNER = (
-    600, 500, 301, 202, 112, 110, 111, 600, 114, 402, 210, 410, 212, 312, 303, 310, 203, 200,
-    113, 600, 311, 313, 120, 400, 403, 302, 600, 201, 211, 121, 321, 401, 122, 300, 123, 320,
-    700, 323, 124, 322, 213, 701, 413, 222, 411, 702, 412, 422, 703, 704, 220, 223, 221, 705,
-    420, 421, 423, 706, 707,
+    303, 110, 112, 111, 500, 210, 312, 113, 410, 600, 310, 114, 200, 202, 212, 120, 201, 302,
+    402, 211, 600, 401, 203, 121, 320, 301, 600, 321, 123, 313, 300, 122, 403, 600, 311, 400,
+    323, 411, 700, 322, 124, 213, 701, 412, 413, 702, 703, 223, 222, 422, 220, 221, 704, 421,
+    420, 705, 423, 706, 707,
 )
 
 
 def step_kernel(
-    ctx_count, owned, units, picks_ref, lengths_ref, queries_ref, cache_ref, out_ref,
-    raw_q, near_cache, q_ref, flags_ref, all_flags, gath, pool, tails, keys, positions, listed_v, listed,
+    ctx_count, owned, units, picks_hbm, lengths_hbm, queries_ref, cache_ref, out_ref,
+    picks_ref, lengths_ref, raw_q, near_cache, near, near_tails, q_ref, flags_ref, all_flags, gath, pool, tails, keys, positions, listed_v, listed,
     top_ref, total_ref, acc_ref, s_a, s_b, p_a, p_b, h_a, h_b,
-    q_sem, cache_sem, list_sem, flag_send, flag_recv, send, recv,
+    picks_sem, lengths_sem, q_sem, cache_sem, list_sem, flag_send, flag_recv, send, recv,
 ):
     rows, feature, heads = queries_ref.shape
     rope = feature - LAT
@@ -53,8 +53,9 @@
 
     fetch = pltpu.make_async_copy(queries_ref, raw_q, q_sem)
     fetch_cache = pltpu.make_async_copy(cache_ref, near_cache, cache_sem)
-    fetch_cache.start()
-    fetch.start()
+    fetch_picks = pltpu.make_async_copy(picks_hbm, picks_ref, picks_sem)
+    fetch_lengths = pltpu.make_async_copy(lengths_hbm, lengths_ref, lengths_sem)
+    fetch_picks.start()
 
     def at(zz, yy, cc):
         return (zz * 2 + yy) * 2 + cc
@@ -67,6 +68,10 @@
             barrier, inc=1, device_id={"ctx": lax.rem(me + d, ctx_count)}, device_id_type=MESH
         )
 
+    fetch_cache.start()
+    fetch_lengths.start()
+    fetch.start()
+    fetch_picks.wait()
     flag_rows = flags_ref.shape[0]
     block_id = lax.broadcasted_iota(jnp.int32, (flag_rows, LANES), 0) * LANES
     block_id += lax.broadcasted_iota(jnp.int32, (flag_rows, LANES), 1)
@@ -135,6 +140,20 @@
             begin[v] += here
         ordered = jnp.where(lane == place, picks_ref[0, k], ordered)
 
+    fetch_cache.wait()
+
+    @pl.loop(0, owned // 2)
+    def _(b):
+        tokens = near_cache[:, pl.ds(pl.multiple_of(b * pair, pair), pair)].T
+        tail = tokens[:, LAT:]
+        packed = jnp.concatenate(
+            [tail[i * tall : (i + 1) * tall, :] for i in range(pair // tall)], axis=1
+        )
+        near[2 * b] = tokens[:BLOCK, :LAT]
+        near[2 * b + 1] = tokens[BLOCK:, :LAT]
+        near_tails[2 * b] = packed[:, : LAT // 2]
+        near_tails[2 * b + 1] = packed[:, LAT // 2 :]
+
     @pl.loop(1, ctx_count)
     def _(d):
         flag_arrival(lax.rem(me + d, ctx_count)).wait_recv()
@@ -204,9 +223,6 @@
         tails[slot] = gath[slot, pair:]
 
     past = ctx_count * owned
-    fetch_cache.wait()
-    token = lax.broadcasted_iota(jnp.int32, (pair, owned * BLOCK), 0)
-    column = lax.broadcasted_iota(jnp.int32, (pair, owned * BLOCK), 1)
     starts = []
     last = jnp.int32(-1)
 
@@ -216,22 +232,12 @@
     for u in [v for r in range(span) for v in range(r, units, span)]:
         while len(starts) < 2 * u + 2:
             last = jnp.min(jnp.where(mine & (block_id > last), block_id, past))
-            starts.append(jnp.minimum(last - me * owned, owned - 1) * BLOCK)
-        first, second = starts[2 * u], starts[2 * u + 1]
-        wanted = jnp.where(token < BLOCK, first + token, second + token - BLOCK)
-        chosen = jnp.where(column == wanted, 1.0, 0.0).astype(jnp.bfloat16)
-        tokens = lax.dot_general(
-            chosen, near_cache[...], (((1,), (1,)), ((), ())), preferred_element_type=jnp.float32
-        ).astype(jnp.bfloat16)
-        tail = tokens[:, LAT:]
-        packed = jnp.concatenate(
-            [tail[i * tall : (i + 1) * tall, :] for i in range(pair // tall)], axis=1
-        )
-        gath[me * units + u, :pair, :] = tokens[:, :LAT]
-        gath[me * units + u, pair:, :] = packed
-        pool[2 * (me * units + u)] = tokens[:BLOCK, :LAT]
-        pool[2 * (me * units + u) + 1] = tokens[BLOCK:, :LAT]
-        tails[me * units + u] = packed
+            starts.append(jnp.minimum(last - me * owned, owned - 1))
+        unit = me * units + u
+        for h in range(2):
+            block = starts[2 * u + h]
+            gath[unit, h * BLOCK : (h + 1) * BLOCK, :] = near[block]
+            gath[unit, pair:, h * LAT // 2 : (h + 1) * LAT // 2] = near_tails[block]
         if units == 1:
             forward(z, jnp.int32(0))
         else:
@@ -249,6 +255,10 @@
             @pl.when(core != path)
             def _():
                 unit_copy(me * units + u, other_path(u), 3, sibling).start()
+
+    @pl.loop(0, units)
+    def _(u):
+        keep(me * units + u)
 
     if units > 1:
         @pl.loop(0, units)
@@ -531,6 +541,7 @@
                 batch.append(w)
 
     listing.wait()
+    fetch_lengths.wait()
     if scripted:
         for n in range(8):
             pl.when(edge)(lambda: emit(pieces(EDGE, n), False))
@@ -576,22 +587,26 @@
     rows, heads, feature = queries.shape
     owned = latent_cache.shape[0] // BLOCK
     units = max(1, 2 * TOPK // ctx_count)
-    flag_rows = -(-(ctx_count * owned) // LANES // 8) * 8
+    flag_rows = -(-(ctx_count * owned) // LANES)
     tall = 2 * BLOCK + 2 * BLOCK * (feature - LAT) // LAT
     height = (4 if rows % 4 == 0 else 1) * heads
     return pl.pallas_call(
         functools.partial(step_kernel, ctx_count, owned, units),
         out_shape=pltpu.VMEM((rows, heads, LAT), jnp.bfloat16),
         in_specs=[
-            pl.BlockSpec(memory_space=pltpu.SMEM),
-            pl.BlockSpec(memory_space=pltpu.SMEM),
+            pl.BlockSpec(memory_space=pl.ANY),
+            pl.BlockSpec(memory_space=pl.ANY),
             pl.BlockSpec(memory_space=pl.ANY),
             pl.BlockSpec(memory_space=pl.ANY),
         ],
         out_specs=pl.BlockSpec(memory_space=pltpu.VMEM),
         scratch_shapes=[
+            pltpu.SMEM((1, TOPK), jnp.int32),
+            pltpu.SMEM((rows,), jnp.int32),
             pltpu.VMEM((rows, feature, heads), jnp.bfloat16),
             pltpu.VMEM((feature, owned * BLOCK), jnp.bfloat16),
+            pltpu.VMEM((owned, BLOCK, LAT), jnp.bfloat16),
+            pltpu.VMEM((owned, tall - 2 * BLOCK, LAT // 2), jnp.bfloat16),
             pltpu.VMEM((rows, heads, feature), jnp.bfloat16),
             pltpu.VMEM((flag_rows, LANES), jnp.int32),
             pltpu.VMEM((ctx_count, flag_rows, LANES), jnp.int32),
@@ -608,9 +623,7 @@
             *[pltpu.VMEM((height, CHUNK * BLOCK), jnp.float32)] * 2,
             *[pltpu.VMEM((height, CHUNK * BLOCK), jnp.bfloat16)] * 2,
             *[pltpu.VMEM((height, 1), jnp.float32)] * 2,
-            pltpu.SemaphoreType.DMA,
-            pltpu.SemaphoreType.DMA,
-            pltpu.SemaphoreType.DMA,
+            *[pltpu.SemaphoreType.DMA] * 5,
             pltpu.SemaphoreType.DMA((ctx_count,)),
             pltpu.SemaphoreType.DMA((ctx_count,)),
             pltpu.SemaphoreType.DMA((ctx_count // 2 * units, 4)),

time: 68.5 us -> 66.9 us (0.977)
  Pallas kernels: 66.8 us -> 65.5 us
    pallas_call x1, Pallas kernels: 66.8 us -> 65.5 us  [shards(): pl.pallas_call(functools.partial(step_kernel, ctx_count, owned, units), o...]
where the time goes in v4:
time: 66.9 us; the launch traced here: 66.8 us
  Pallas kernels  65.5 us (98%)
  local copies, waits for them, and re-layouts  1.32 us (2%)
    pallas_call x1, Pallas kernels, shards(): pl.pallas_call(functools.partial(step_kernel, ctx_count, owned, units), o...  65.5 us

profile of v4, /device:TPU:0, one launch (start us, length us, event | category | flops | bytes accessed | tf_op | source)
XLA Modules:
  0.0 66.8 jit_solution(13110891836640464131)
XLA Ops:
  0.0 65.5 %shard_map.46 = bf16[16,128,512]{2,1,0:T(8,128)(2,1)S(1)} custom-call(s32[1,32]{1,0:T(1,128)} %picks_hbm.1, s32[16]{0:T(128)} %lengths_hbm.1, bf16[16,576,128]{2,1,0:T(8,128)(2,1)} %bitcast.2, bf16[576,1024]{1,0:T(8,128)(2,1)} %bitcast.3), custom_call_target="tpu_custom_call" | custom-call | tf_op jit(solution)/shard_map/pallas_call | solution.py:593
  65.5 1.3 %copy.6 = bf16[16,128,512]{2,1,0:T(8,128)(2,1)} copy(bf16[16,128,512]{2,1,0:T(8,128)(2,1)S(1)} %shard_map.46) | data formatting | bytes 4194304

commit v5 on v4

--- a/solution.py
+++ b/solution.py
@@ -62,7 +62,7 @@
 
     barrier = pltpu.get_barrier_semaphore()
 
-    @pl.loop(1, ctx_count)
+    @pl.loop(1, ctx_count, unroll=ctx_count - 1 < 16)
     def _(d):
         pl.semaphore_signal(
             barrier, inc=1, device_id={"ctx": lax.rem(me + d, ctx_count)}, device_id_type=MESH
@@ -103,7 +103,7 @@
             device_id_type=MESH,
         )
 
-    @pl.loop(1, ctx_count)
+    @pl.loop(1, ctx_count, unroll=ctx_count - 1 < 16)
     def _(d):
         flag_copy(d).start()
 

time: 66.9 us -> 66.9 us (level)
  no operation moved by 1% of the time
where the time goes in v5:
time: 66.9 us; the launch traced here: 66.7 us
  Pallas kernels  65.4 us (98%)
  local copies, waits for them, and re-layouts  1.32 us (2%)
    pallas_call x1, Pallas kernels, shards(): pl.pallas_call(functools.partial(step_kernel, ctx_count, owned, units), o...  65.4 us

profile of v5, /device:TPU:0, one launch (start us, length us, event | category | flops | bytes accessed | tf_op | source)
XLA Modules:
  0.0 66.7 jit_solution(3659983343370275673)
XLA Ops:
  0.0 65.4 %shard_map.46 = bf16[16,128,512]{2,1,0:T(8,128)(2,1)S(1)} custom-call(s32[1,32]{1,0:T(1,128)} %picks_hbm.1, s32[16]{0:T(128)} %lengths_hbm.1, bf16[16,576,128]{2,1,0:T(8,128)(2,1)} %bitcast.2, bf16[576,1024]{1,0:T(8,128)(2,1)} %bitcast.3), custom_call_target="tpu_custom_call" | custom-call | tf_op jit(solution)/shard_map/pallas_call | solution.py:593
  65.4 1.3 %copy.6 = bf16[16,128,512]{2,1,0:T(8,128)(2,1)} copy(bf16[16,128,512]{2,1,0:T(8,128)(2,1)S(1)} %shard_map.46) | data formatting | bytes 4194304
